TPU v7x, 32 devices: a whole 2x2x4 slice. The times are simulated.
32 devices in a mesh: dp: 2 (over x), ep: 16 (over z, y, core).
Axes of the slice: x: 2, y: 2, z: 4, core: 2. Of those that a mesh axis runs over, the one named last changes fastest.
Arguments:
- dy_home: bfloat16 [4096, 1024], P(('dp', 'ep')), parts along dimension 0
- topk_idx: int32 [4096, 8], P(('dp', 'ep')), parts along dimension 0
- slot_idx: int32 [4096, 8], P(('dp', 'ep')), parts along dimension 0
- gates: float32 [4096, 8], P(('dp', 'ep')), parts along dimension 0
- y_back: bfloat16 [4096, 8, 1024], P(('dp', 'ep')), parts along dimension 0
- x_disp: bfloat16 [64, 1024, 1024], P(('dp', 'ep')), parts along dimension 0
- h1_disp: bfloat16 [64, 1024, 512], P(('dp', 'ep')), parts along dimension 0
- h3_disp: bfloat16 [64, 1024, 512], P(('dp', 'ep')), parts along dimension 0
- w_gate: bfloat16 [32, 1024, 512], P('ep')
- w_up: bfloat16 [32, 1024, 512], P('ep')
- w_down: bfloat16 [32, 512, 1024], P('ep')
Outputs:
- output 1: bfloat16 [4096, 1024], P(('dp', 'ep')), parts along dimension 0
- output 2: float32 [4096, 8], P(('dp', 'ep')), parts along dimension 0
- output 3: float32 [64, 1024, 512], P(('dp', 'ep')), parts along dimension 0
- output 4: float32 [64, 1024, 512], P(('dp', 'ep')), parts along dimension 0
- output 5: float32 [64, 512, 1024], P(('dp', 'ep')), parts along dimension 0
There are 2 independent parts. A program takes and returns all parts, laid end to end along the dimension named above; an argument that names none is the same for every part.
All inputs are finite; a program needn't handle non-finite values.
Results may differ from a plain program's by a relative error of at most 0.0149638.
Values are sent between devices in bfloat16 or wider.
A program may use at most 1 GiB of HBM per device.

v0:
```python
import jax
import jax.numpy as jnp
from jax import lax
from jax.sharding import PartitionSpec as P


def gated_buffer(dy_rows, gates, flat_pos, rows_all):
    num_choice = flat_pos.size
    choice_of = jnp.full((rows_all,), num_choice, jnp.int32).at[flat_pos.reshape(-1)].set(
        jnp.arange(num_choice, dtype=jnp.int32), mode='drop')
    gate_pad = jnp.concatenate([gates.reshape(-1), jnp.zeros((1,), jnp.float32)])
    row_gate = gate_pad[choice_of]
    row_tok = jnp.minimum(choice_of // gates.shape[1], dy_rows.shape[0] - 1)
    row_dy = jnp.take(dy_rows, row_tok, axis=0)
    return (row_gate[:, None] * row_dy.astype(jnp.float32)).astype(jnp.bfloat16)


def expert_backward(dy_disp, x_disp, h_gate, h_up, w_gate, w_up, w_down):
    gate_f = h_gate.astype(jnp.float32)
    up_f = h_up.astype(jnp.float32)
    sig_gate = jax.nn.sigmoid(gate_f)
    silu_g = gate_f * sig_gate
    hidden_act = (silu_g * up_f).astype(jnp.bfloat16)
    d_act = jnp.einsum('erd,efd->erf', dy_disp, w_down, preferred_element_type=jnp.float32).astype(jnp.bfloat16).astype(jnp.float32)
    dh_gate = (d_act * up_f * sig_gate * (1.0 + gate_f * (1.0 - sig_gate))).astype(jnp.bfloat16)
    dh_up = (d_act * silu_g).astype(jnp.bfloat16)
    dw_down = jnp.einsum('erf,erd->efd', hidden_act, dy_disp, preferred_element_type=jnp.float32)
    dw_gate = jnp.einsum('erd,erf->edf', x_disp, dh_gate, preferred_element_type=jnp.float32)
    dw_up = jnp.einsum('erd,erf->edf', x_disp, dh_up, preferred_element_type=jnp.float32)
    dx_disp = (jnp.einsum('erf,edf->erd', dh_gate, w_gate, preferred_element_type=jnp.float32)
               + jnp.einsum('erf,edf->erd', dh_up, w_up, preferred_element_type=jnp.float32)).astype(jnp.bfloat16)
    return dx_disp, dw_gate, dw_up, dw_down


def solution(mesh):
    ep_size = mesh.shape['ep']
    tok_spec = P(('dp', 'ep'), None)
    buf_spec = P(('dp', 'ep'), None, None)
    expert_spec = P('ep', None, None)

    def device_step(dy_loc, topk_idx, slot_idx, gates, y_back, x_disp, h1_disp, h3_disp, w_gate, w_up, w_down):
        num_experts = w_gate.shape[0] * ep_size
        capacity = x_disp.shape[1] // ep_size
        d_model = dy_loc.shape[1]
        rows_all = num_experts * capacity
        d_gates = jnp.einsum('td,tjd->tj', dy_loc, y_back, preferred_element_type=jnp.float32)
        flat_pos = jnp.where(slot_idx >= 0, topk_idx * capacity + slot_idx, rows_all)
        send_buf = gated_buffer(dy_loc, gates, flat_pos, rows_all).reshape(num_experts, capacity, d_model)
        dy_disp = lax.all_to_all(send_buf, 'ep', 0, 1, tiled=True)
        dx_disp, dw_gate, dw_up, dw_down = expert_backward(dy_disp, x_disp, h1_disp, h3_disp, w_gate, w_up, w_down)
        dx_buf = lax.all_to_all(dx_disp, 'ep', 1, 0, tiled=True).reshape(rows_all, d_model)
        returned = jnp.take(dx_buf, flat_pos, axis=0, mode='fill', fill_value=0)
        dx_loc = jnp.sum(returned, axis=1, dtype=jnp.float32).astype(jnp.bfloat16)
        return dx_loc, d_gates, dw_gate, dw_up, dw_down

    return jax.shard_map(
        device_step, mesh=mesh,
        in_specs=(tok_spec, tok_spec, tok_spec, tok_spec, buf_spec, buf_spec, buf_spec, buf_spec,
                  expert_spec, expert_spec, expert_spec),
        out_specs=(tok_spec, tok_spec, buf_spec, buf_spec, buf_spec),
        check_vma=False)
```

profile of v0, /device:TPU:13, one launch (start us, length us, event | category | flops | bytes accessed | tf_op | source)
XLA Modules:
  0.0 267.6 jit_solution(17132166972248899274)
XLA Ops:
  0.6 0.9 compare_and_fusion.1
  1.7 4.3 %scatter_custom_fusion = s32[2048]{0:T(1024)S(1)} fusion(s32[1024]{0:T(1024)S(1)} %bitcast.35, s32[1024]{0:T(1024)S(1)} %iota.3, s32[]{:T(128)} %constant.34.clone.1), kind=kCustom, calls=%fused_computation.45 | custom fusion | bytes 8196 | tf_op jit(solution)/shard_map/scatter | solution.py:9
  6.1 0.8 copy.35
  7.0 11.8 %gather_fusion = f32[2048]{0:T(1024)S(1)} fusion(f32[1025]{0:T(1024)S(1)} %pad_maximum_fusion, s32[2048]{0:T(1024)S(1)} %get-tuple-element.22), kind=kCustom, calls=%fused_computation | custom fusion | bytes 24576 | tf_op jit(solution)/shard_map/gather | solution.py:12
  19.0 9.6 %gather_fusion.1 = bf16[2048,1024]{1,0:T(8,128)(2,1)} fusion(bf16[128,1024]{1,0:T(8,128)(2,1)S(1)} %copy-done.2, s32[2048]{0:T(1024)S(1)} %get-tuple-element.23), kind=kCustom, calls=%fused_computation.1 | custom fusion | bytes 8396800 | tf_op jit(solution)/shard_map/jit(_take)/gather | solution.py:14
  28.6 2.8 %multiply_convert_fusion = bf16[32,64,1024]{2,1,0:T(8,128)(2,1)S(1)} fusion(bf16[32,64,1024]{2,1,0:T(8,128)(2,1)} %bitcast.30, f32[32,64]{1,0:T(8,128)S(1)} %mul.40, pred[32,64]{1,0:T(8,128)(4,1)S(1)} %broadcast_in_dim.42), kind=kLoop, calls=%fused_computation.5 | loop fusion | flops 8388608 | bytes 8398848 | tf_op jit(solution)/shard_map/convert_element_type | solution.py:15
  31.4 98.5 %all_to_all.33 = bf16[32,64,1024]{2,1,0:T(8,128)(2,1)S(1)} all-to-all(bf16[32,64,1024]{2,1,0:T(8,128)(2,1)S(1)} %multiply_convert_fusion), channel_id=1, replica_groups=mesh['dp'=2,'ep'=16] {'ep'}, dimensions={0} | all-to-all | bytes 8388608 | tf_op jit(solution)/shard_map/all_to_all | solution.py:49
  129.8 0.7 copy.37
  130.6 2.0 copy-done.3
  132.5 2.4 convolution_convert_fusion
  135.0 3.2 %fusion.24 = f32[2,1024,1024]{2,1,0:T(8,128)S(1)} fusion(bf16[2,1024,512]{2,1,0:T(8,128)(2,1)S(1)} %copy-done, bf16[2,1024,512]{2,1,0:T(8,128)(2,1)S(1)} %copy-done.6, bf16[2,1024,512]{2,1,0:T(8,128)(2,1)S(1)} %convolution_convert_fusion, bf16[2,1024,512]{2,1,0:T(8,128)(2,1)S(1)} %copy-done.8), kind=kOutput, calls=%fused_computation.51 | convolution fusion | flops 2161115136 | bytes 16777216 | tf_op jit(solution)/shard_map/erf,edf->erd/dot_general | solution.py:30
  138.2 4.8 %add_convert_fusion = bf16[2,1024,1024]{2,1,0:T(8,128)(2,1)} fusion(f32[2,1024,1024]{2,1,0:T(8,128)S(1)} %fusion.24, bf16[2,1024,512]{2,1,0:T(8,128)(2,1)S(1)} %copy-done.5, bf16[2,1024,512]{2,1,0:T(8,128)(2,1)S(1)} %convolution_convert_fusion, bf16[2,1024,512]{2,1,0:T(8,128)(2,1)S(1)} %copy-done.8), kind=kOutput, calls=%fused_computation.4 | convolution fusion | flops 2160066560 | bytes 18874368 | tf_op jit(solution)/shard_map/erf,edf->erd/dot_general | solution.py:31
  142.9 8.7 %copy.38 = bf16[2,1024,1024]{2,0,1:T(2,128)(2,1)} copy(bf16[2,1024,1024]{2,1,0:T(8,128)(2,1)} %add_convert_fusion) | data formatting | bytes 8388608 | tf_op jit(solution)/shard_map/convert_element_type | solution.py:31
  151.6 5.4 %all-to-all-start.1 = ((bf16[2,1024,1024]{2,0,1:T(2,128)(2,1)}), bf16[2,1024,1024]{2,0,1:T(2,128)(2,1)}, u32[]{:S(2)}, u32[]{:S(2)}) async-start(bf16[2,1024,1024]{2,0,1:T(2,128)(2,1)} %copy.38), calls=%async_computation.1 | async-start | bytes 8388608 | tf_op jit(solution)/shard_map/all_to_all | solution.py:51
  157.4 3.0 %fusion.12 = f32[128,1,8]{2,1,0:T(1,128)S(1)} fusion(bf16[128,8,1024]{2,1,0:T(8,128)(2,1)} %param.15, bf16[128,1024,1]{1,0,2:T(8,128)(2,1)S(1)} %bitcast.28), kind=kOutput, calls=%fused_computation.27 | convolution fusion | flops 2097152 | bytes 2363392 | tf_op jit(solution)/shard_map/td,tjd->tj/dot_general | solution.py:46
  161.0 9.1 %convolution_bitcast_fusion.1 = f32[2,1024,512]{1,2,0:T(8,128)} fusion(bf16[2,1024,1024]{2,1,0:T(8,128)(2,1)} %param.16, bf16[2,1024,512]{2,1,0:T(8,128)(2,1)} %param.18, bf16[2,1024,512]{2,1,0:T(8,128)(2,1)} %copy-done.10, bf16[2,1024,512]{2,1,0:T(8,128)(2,1)} %param.17), kind=kOutput, calls=%fused_computation.22 | convolution fusion | flops 2161115136 | bytes 14680064 | tf_op jit(solution)/shard_map/erd,erf->edf/dot_general | solution.py:28
  170.1 5.5 %copy.44 = f32[2,1024,512]{2,1,0:T(8,128)} copy(f32[2,1024,512]{1,2,0:T(8,128)} %convolution_bitcast_fusion.1) | data formatting | bytes 8388608
  175.6 7.4 %convolution_bitcast_fusion = f32[2,1024,512]{1,2,0:T(8,128)} fusion(bf16[2,1024,1024]{2,1,0:T(8,128)(2,1)} %param.16, bf16[2,1024,512]{2,1,0:T(8,128)(2,1)} %copy-done.10, bf16[2,1024,512]{2,1,0:T(8,128)(2,1)S(1)} %copy-done.9), kind=kOutput, calls=%fused_computation.21 | convolution fusion | flops 2155872256 | bytes 12582912 | tf_op jit(solution)/shard_map/erd,erf->edf/dot_general | solution.py:29
  183.0 5.5 %copy.45 = f32[2,1024,512]{2,1,0:T(8,128)} copy(f32[2,1024,512]{1,2,0:T(8,128)} %convolution_bitcast_fusion) | data formatting | bytes 8388608
  188.5 7.4 %fusion.9 = f32[2,512,1024]{2,1,0:T(8,128)} fusion(bf16[2,1024,1024]{2,1,0:T(8,128)(2,1)} %bitcast.33, bf16[2,1024,512]{2,1,0:T(8,128)(2,1)S(1)} %copy-done.7, bf16[2,1024,512]{2,1,0:T(8,128)(2,1)} %param.17), kind=kOutput, calls=%fused_computation.23 | convolution fusion | flops 2155872256 | bytes 12582912 | tf_op jit(solution)/shard_map/erf,erd->efd/dot_general | solution.py:27
  195.9 53.9 %all-to-all-done.1 = bf16[2,1024,1024]{2,0,1:T(2,128)(2,1)} async-done(((bf16[2,1024,1024]{2,0,1:T(2,128)(2,1)}), bf16[2,1024,1024]{2,0,1:T(2,128)(2,1)}, u32[]{:S(2)}, u32[]{:S(2)}) %all-to-all-start.1) | async-done | bytes 4194336 | tf_op jit(solution)/shard_map/all_to_all | solution.py:51
  249.7 5.5 %copy.39 = bf16[2,16,64,1024]{3,2,0,1:T(8,128)(2,1)} copy(bf16[2,16,64,1024]{3,0,2,1:T(2,128)(2,1)} %bitcast.5) | data formatting | bytes 8388608 | tf_op jit(solution)/shard_map/all_to_all | solution.py:51
  255.3 8.9 %gather_fusion.2 = bf16[1024,1024]{1,0:T(8,128)(2,1)} fusion(bf16[2048,1024]{1,0:T(8,128)(2,1)} %bitcast.29, s32[1024]{0:T(1024)S(1)} %broadcast_clamp_fusion.1), kind=kCustom, calls=%fused_computation.2 | custom fusion | bytes 4198400 | tf_op jit(solution)/shard_map/jit(_take)/gather | solution.py:52
  264.2 3.4 %fusion.11 = bf16[128,1024]{1,0:T(8,128)(2,1)} fusion(bf16[1024,1024]{1,0:T(8,128)(2,1)} %gather_fusion.2, pred[128,8]{1,0:T(8,128)(4,1)S(1)} %copy.34), kind=kLoop, calls=%fused_computation.25 | loop fusion | flops 1966080 | bytes 2360320 | tf_op jit(solution)/shard_map/reduce_sum | solution.py:53
  (37 shorter events, 1.5 us)
Async XLA Ops:
  0.6 134.3 %copy-start = (bf16[2,1024,512]{2,1,0:T(8,128)(2,1)S(1)}, bf16[2,1024,512]{2,1,0:T(8,128)(2,1)}, u32[]{:S(2)}) copy-start(bf16[2,1024,512]{2,1,0:T(8,128)(2,1)} %param.19) | copy-start | bytes 6291460
  7.0 12.0 %copy-start.2 = (bf16[128,1024]{1,0:T(8,128)(2,1)S(1)}, bf16[128,1024]{1,0:T(8,128)(2,1)}, u32[]{:S(2)}) copy-start(bf16[128,1024]{1,0:T(8,128)(2,1)} %param.11) | copy-start | bytes 786436
  129.8 2.7 %copy-start.4 = (bf16[2,512,1024]{2,1,0:T(8,128)(2,1)S(1)}, bf16[2,512,1024]{2,1,0:T(8,128)(2,1)}, u32[]{:S(2)}) copy-start(bf16[2,512,1024]{2,1,0:T(8,128)(2,1)} %param.21) | copy-start | bytes 6291460
  130.6 2.0 copy-start.3
  132.5 2.4 copy-start.6
  132.5 2.4 copy-start.8
  134.9 3.2 %copy-start.10 = (bf16[2,1024,512]{2,1,0:T(8,128)(2,1)}, bf16[2,1024,512]{2,1,0:T(8,128)(2,1)S(1)}, u32[]{:S(2)}) copy-start(bf16[2,1024,512]{2,1,0:T(8,128)(2,1)S(1)} %convolution_convert_fusion) | copy-start | bytes 6291460
  134.9 3.2 %copy-start.5 = (bf16[2,1024,512]{2,1,0:T(8,128)(2,1)S(1)}, bf16[2,1024,512]{2,1,0:T(8,128)(2,1)}, u32[]{:S(2)}) copy-start(bf16[2,1024,512]{2,1,0:T(8,128)(2,1)} %param.20) | copy-start | bytes 6291460
  151.6 98.1 %all-to-all-start.1 = ((bf16[2,1024,1024]{2,0,1:T(2,128)(2,1)}), bf16[2,1024,1024]{2,0,1:T(2,128)(2,1)}, u32[]{:S(2)}, u32[]{:S(2)}) async-start(bf16[2,1024,1024]{2,0,1:T(2,128)(2,1)} %copy.38), calls=%async_computation.1 | async-start | bytes 8388608 | tf_op jit(solution)/shard_map/all_to_all | solution.py:51
  170.1 5.5 %copy-start.9 = (bf16[2,1024,512]{2,1,0:T(8,128)(2,1)S(1)}, bf16[2,1024,512]{2,1,0:T(8,128)(2,1)}, u32[]{:S(2)}) copy-start(bf16[2,1024,512]{2,1,0:T(8,128)(2,1)} %param.17) | copy-start | bytes 6291460
  183.0 5.5 %copy-start.7 = (bf16[2,1024,512]{2,1,0:T(8,128)(2,1)S(1)}, bf16[2,1024,512]{2,1,0:T(8,128)(2,1)}, u32[]{:S(2)}) copy-start(bf16[2,1024,512]{2,1,0:T(8,128)(2,1)} %param.18) | copy-start | bytes 6291460
  255.3 12.3 %copy-start.1 = (bf16[2,1024,512]{2,1,0:T(8,128)(2,1)S(1)}, bf16[2,1024,512]{2,1,0:T(8,128)(2,1)}, u32[]{:S(2)}) copy-start(bf16[2,1024,512]{2,1,0:T(8,128)(2,1)} %param.19) | copy-start | bytes 6291460
where the time goes:
time: 268 us
  blocking collectives  98.5 us (37%)
  local copies, waits for them, and re-layouts  64.8 us (24%)
  waiting for transfers between devices  53.9 us (20%)
  matrix products  37.1 us (14%)
  other arithmetic  7.14 us (3%)
  starting transfers between devices  5.43 us (2%)
    all_to_all x1, blocking collectives, device_step(): dy_disp = lax.all_to_all(send_buf, 'ep', 0, 1, tiled=True)  98.5 us
    all_to_all x1, waiting for transfers between devices, device_step(): lax.all_to_all(dx_disp, 'ep', 1, 0, tiled=True).reshape(rows_all, d_model)  53.9 us
    unnamed x25, local copies, waits for them, and re-layouts  13.8 us
    gather x1, local copies, waits for them, and re-layouts, gated_buffer(): row_gate = gate_pad[choice_of]  11.8 us
    gather x1, local copies, waits for them, and re-layouts, gated_buffer(): row_dy = jnp.take(dy_rows, row_tok, axis=0)  9.61 us
    dot_general x1, matrix products, expert_backward(): jnp.einsum('erd,erf->edf', x_disp, dh_gate, preferred_element_type=jnp.fl...  9.1 us
    gather x1, local copies, waits for them, and re-layouts, device_step(): returned = jnp.take(dx_buf, flat_pos, axis=0, mode='fill', fill_value=0)  8.91 us
    convert_element_type x1, local copies, waits for them, and re-layouts, expert_backward(): dx_disp = (jnp.einsum('erf,edf->erd', dh_gate, w_gate, preferred_element_...  8.69 us
  transfers between devices with their start and end apart: 1, of which 1 were waited for; matrix products, arithmetic and copies ran while one was open for 15% of the time, Pallas kernels for 0%

commit v1 on v0

v1 whole, which is shorter than its diff:
```python
import functools

import jax
import jax.numpy as jnp
from jax import lax
from jax.experimental import pallas as pl
from jax.experimental.pallas import tpu as pltpu
from jax.sharding import PartitionSpec as P

MESH = pl.DeviceIdType.MESH
F32 = jnp.float32
BF16 = jnp.bfloat16
NZ = 4
NR = 2


def line_pos(z, k):
    edge = z * (3 - z) // 2
    far = z // 2
    is0 = (3 - k) // 3
    is1 = (k + 2) // 3 - (k + 1) // 3
    q = k + edge * is0 - edge * is1
    return q + 3 * far - 2 * far * q


def dot_t(a, b):
    return lax.dot_general(a, b, (((1,), (1,)), ((), ())), preferred_element_type=F32)


def exchange_kernel(tok, cap, top,
                    dy_ref, meta_ref, h1_hbm, h3_hbm, wg_hbm, wu_hbm, wd_hbm,
                    dx_ref, dyd_hbm, act_hbm, dh1_hbm, dh3_hbm,
                    gat, met, h1, h3, wg, wu, wd, dyd, act, dh1, dh3, xd, xr,
                    own, sy, ry, sz, rz,
                    load_sem, out_sem, ag_send, ag_recv, mt_send, mt_recv,
                    xs_sem, xr_sem, sy_sem, ry_sem, sz_sem, rz_sem):
    me = lax.axis_index('ep')
    dp = lax.axis_index('dp')
    z, y, c = me // 4, (me // 2) % 2, me % 2
    oy, oc = 1 - y, 1 - c

    def dev(z_, y_, c_):
        return (dp, (z_ * 2 + y_) * 2 + c_)

    def home(z_, y_, c_):
        return (z_ * 2 + y_) * 2 + c_

    loads = [pltpu.make_async_copy(s, d, load_sem.at[i]) for i, (s, d) in enumerate(
        ((wd_hbm, wd), (h1_hbm, h1), (h3_hbm, h3), (wg_hbm, wg), (wu_hbm, wu)))]
    for cp in loads:
        cp.start()

    barrier = pltpu.get_barrier_semaphore()
    pl.semaphore_signal(barrier, inc=1, device_id=dev(z, y, oc), device_id_type=MESH)
    pl.semaphore_signal(barrier, inc=1, device_id=dev(z, oy, c), device_id_type=MESH)

    @pl.when(z > 0)
    def _():
        pl.semaphore_signal(barrier, inc=1, device_id=dev(z - 1, y, c), device_id_type=MESH)

    @pl.when(z < NZ - 1)
    def _():
        pl.semaphore_signal(barrier, inc=1, device_id=dev(z + 1, y, c), device_id_type=MESH)

    pl.semaphore_wait(barrier, 3 + z * (NZ - 1 - z) // 2)

    def ag_copies(src, msrc, hid, way, target):
        return (pltpu.make_async_remote_copy(src, gat.at[hid], ag_send.at[hid, way], ag_recv.at[hid],
                                             device_id=target, device_id_type=MESH),
                pltpu.make_async_remote_copy(msrc, met.at[hid], mt_send.at[hid, way], mt_recv.at[hid],
                                             device_id=target, device_id_type=MESH))

    def start(copies):
        for cp in copies:
            cp.start()

    def ag_wait(hid):
        for cp in ag_copies(gat.at[hid], met.at[hid], hid, 0, dev(z, y, oc)):
            cp.wait_recv()

    @pl.when(z < NZ - 1)
    def _():
        start(ag_copies(dy_ref, meta_ref, me, 2, dev(z + 1, y, c)))

    @pl.when(z > 0)
    def _():
        start(ag_copies(dy_ref, meta_ref, me, 3, dev(z - 1, y, c)))

    start(ag_copies(dy_ref, meta_ref, me, 1, dev(z, oy, c)))
    start(ag_copies(dy_ref, meta_ref, me, 0, dev(z, y, oc)))
    gat[me] = dy_ref[...]
    met[me] = meta_ref[...]

    def from_line(k):
        p = line_pos(z, k)
        hid = home(p, y, c)
        ag_wait(hid)
        blk, mblk = gat.at[hid], met.at[hid]

        @pl.when((p < z) & (z < NZ - 1))
        def _():
            start(ag_copies(blk, mblk, hid, 2, dev(z + 1, y, c)))

        @pl.when((p > z) & (z > 0))
        def _():
            start(ag_copies(blk, mblk, hid, 3, dev(z - 1, y, c)))

        start(ag_copies(blk, mblk, hid, 1, dev(z, oy, c)))
        start(ag_copies(blk, mblk, hid, 0, dev(z, y, oc)))

    def from_pair(k):
        hid = home(line_pos(z, k), oy, c)
        ag_wait(hid)
        start(ag_copies(gat.at[hid], met.at[hid], hid, 0, dev(z, y, oc)))

    for cp in loads:
        cp.wait()

    def xs_copy(chip):
        return pltpu.make_async_remote_copy(xd.at[chip, oc], xr.at[chip], xs_sem.at[chip], xr_sem.at[chip],
                                            device_id=dev(z, y, oc), device_id_type=MESH)

    def out_copies(chip):
        rows = pl.ds(chip * 2 * cap, 2 * cap)
        return [pltpu.make_async_copy(s.at[:, rows], d.at[:, rows], out_sem.at[i, chip]) for i, (s, d) in enumerate(
            ((dyd, dyd_hbm), (act, act_hbm), (dh1, dh1_hbm), (dh3, dh3_hbm)))]

    slot = lax.broadcasted_iota(jnp.int32, (cap, 1), 0).astype(F32)

    def group(chip):
        first = (me * 2 * cap).astype(F32)
        rows = pl.ds(chip * 2 * cap, 2 * cap)
        picks, row_gate = [], []
        for e in range(2):
            for h in range(2):
                want = slot + (first + float(e * cap))
                hit = jnp.zeros((cap, tok), F32)
                gsum = jnp.zeros((cap, tok), F32)
                for j in range(top):
                    same = met[chip * 2 + h, j:j + 1, :] == want
                    hit = jnp.where(same, 1.0, hit)
                    gsum = jnp.where(same, met[chip * 2 + h, top + j:top + j + 1, :], gsum)
                row_gate.append(jnp.sum(gsum, axis=1, keepdims=True))
                none = jnp.zeros((cap, tok), F32)
                picks.append(jnp.concatenate([hit, none] if h == 0 else [none, hit], axis=1))
        pick = jnp.concatenate(picks, axis=0).astype(BF16)
        gate = jnp.concatenate(row_gate, axis=0)
        pair = jnp.concatenate([gat[chip * 2], gat[chip * 2 + 1]], axis=0)
        picked = jnp.dot(pick, pair, preferred_element_type=F32)
        rows_dy = (picked * gate).astype(BF16)
        for e in range(2):
            dy_e = rows_dy[e * 2 * cap:(e + 1) * 2 * cap]
            dyd[e, rows] = dy_e
            d_act = dot_t(dy_e, wd[e]).astype(BF16).astype(F32)
            gate_f = h1[e, rows].astype(F32)
            up_f = h3[e, rows].astype(F32)
            sig = jax.nn.sigmoid(gate_f)
            silu = gate_f * sig
            act[e, rows] = (silu * up_f).astype(BF16)
            d1 = (d_act * up_f * sig * (1.0 + gate_f * (1.0 - sig))).astype(BF16)
            d3 = (d_act * silu).astype(BF16)
            dh1[e, rows] = d1
            dh3[e, rows] = d3
            d_x = (dot_t(d1, wg[e]) + dot_t(d3, wu[e])).astype(BF16)
            for h in range(2):
                xd[chip, h, e * cap:(e + 1) * cap] = d_x[h * cap:(h + 1) * cap]
        xs_copy(chip).start()
        for cp in out_copies(chip):
            cp.start()

    def step(n, carry):
        k, side = n // 2, n % 2

        @pl.when((side == 0) & (k < NZ - 1))
        def _():
            from_line(k + 1)
            from_pair(k)

        @pl.when((side == 1) & (k == NZ - 1))
        def _():
            from_pair(k)

        yy = y + side - 2 * y * side
        p = line_pos(z, k)
        ag_wait(home(p, yy, oc))
        group(p * 2 + yy)
        return carry

    lax.fori_loop(0, 2 * NZ, step, 0)

    row_id = lax.broadcasted_iota(jnp.int32, (2 * cap, 1), 0).astype(F32)

    def partial(chip):
        hid = chip * 2 + c
        xs_copy(chip).wait_recv()
        want = jnp.concatenate([row_id + (me * 2 * cap).astype(F32),
                                row_id + ((me + 1 - 2 * c) * 2 * cap).astype(F32)], axis=0)
        hit = jnp.zeros((4 * cap, tok), F32)
        for j in range(top):
            hit = jnp.where(met[hid, j:j + 1, :] == want, 1.0, hit)
        vals = jnp.concatenate([xd[chip, c], xr[chip]], axis=0)
        return lax.dot_general(hit.astype(BF16), vals, (((0,), (0,)), ((), ())), preferred_element_type=F32)

    half = tok // NR

    def y_copy(k, i):
        return pltpu.make_async_remote_copy(sy.at[k, i], ry.at[k, i], sy_sem.at[k, i], ry_sem.at[k, i],
                                            device_id=dev(z, oy, c), device_id_type=MESH)

    def z_copy(k, i, target_z, to_slot):
        return pltpu.make_async_remote_copy(sz.at[k, i], rz.at[to_slot, i], sz_sem.at[k, i], rz_sem.at[to_slot, i],
                                            device_id=dev(target_z, y, c), device_id_type=MESH)

    def z_wait(from_slot, i):
        z_copy(0, i, z, from_slot).wait_recv()

    for k in (3, 2, 1, 0):
        part = partial(line_pos(z, k) * 2 + oy)
        for i in range(NR):
            sy[k, i] = part[i * half:(i + 1) * half]
            y_copy(k, i).start()

    for k in (3, 1, 2):
        p = line_pos(z, k)
        way = jnp.where(p > z, 1, -1)
        own[...] = partial(p * 2 + y)
        behind = z - way
        has_in = (behind >= 0) & (behind < NZ)
        ahead = z + way
        to_slot = jnp.where(ahead == p, jnp.where(way > 0, NZ, NZ + 1), p)
        for i in range(NR):
            y_copy(k, i).wait_recv()
            sz[k, i] = own[i * half:(i + 1) * half] + ry[k, i]

            @pl.when(has_in)
            def _():
                z_wait(p, i)
                sz[k, i] += rz[p, i]

            z_copy(k, i, ahead, to_slot).start()

    own[...] = partial(z * 2 + y)
    for i in range(NR):
        rows = slice(i * half, (i + 1) * half)
        y_copy(0, i).wait_recv()
        own[rows] += ry[0, i]

        @pl.when(z > 0)
        def _():
            z_wait(NZ, i)
            own[rows] += rz[NZ, i]

        @pl.when(z < NZ - 1)
        def _():
            z_wait(NZ + 1, i)
            own[rows] += rz[NZ + 1, i]

        dx_ref[rows] = own[rows].astype(BF16)

    def ag_sent(hid, way):
        for cp in ag_copies(gat.at[hid], met.at[hid], hid, way, dev(z, y, oc)):
            cp.wait_send()

    for k in range(NZ):
        p = line_pos(z, k)
        hid = home(p, y, c)
        ag_sent(hid, 0)
        ag_sent(hid, 1)
        ag_sent(home(p, oy, c), 0)

        @pl.when((p <= z) & (z < NZ - 1))
        def _():
            ag_sent(hid, 2)

        @pl.when((p >= z) & (z > 0))
        def _():
            ag_sent(hid, 3)

        for i in range(NR):
            y_copy(k, i).wait_send()
            if k:
                z_copy(k, i, z, 0).wait_send()

    def drain(chip, carry):
        xs_copy(chip).wait_send()
        for cp in out_copies(chip):
            cp.wait()
        return carry

    lax.fori_loop(0, 2 * NZ, drain, 0)


def exchange(dy, meta, h1, h3, wg, wu, wd, cap, top):
    tok, width = dy.shape
    n_exp, rows, ff = h1.shape
    homes = rows // cap
    chips = homes // 2
    half = tok // NR
    dma = pltpu.SemaphoreType.DMA
    any_spec = pl.BlockSpec(memory_space=pl.ANY)
    vmem_spec = pl.BlockSpec(memory_space=pltpu.VMEM)
    return pl.pallas_call(
        functools.partial(exchange_kernel, tok, cap, top),
        out_shape=(jax.ShapeDtypeStruct((tok, width), BF16),
                   jax.ShapeDtypeStruct((n_exp, rows, width), BF16),
                   jax.ShapeDtypeStruct((n_exp, rows, ff), BF16),
                   jax.ShapeDtypeStruct((n_exp, rows, ff), BF16),
                   jax.ShapeDtypeStruct((n_exp, rows, ff), BF16)),
        in_specs=[vmem_spec] * 2 + [any_spec] * 5,
        out_specs=(vmem_spec,) + (any_spec,) * 4,
        scratch_shapes=[
            pltpu.VMEM((homes, tok, width), BF16),
            pltpu.VMEM((homes, 2 * top, tok), F32),
            pltpu.VMEM(h1.shape, BF16),
            pltpu.VMEM(h3.shape, BF16),
            pltpu.VMEM(wg.shape, BF16),
            pltpu.VMEM(wu.shape, BF16),
            pltpu.VMEM(wd.shape, BF16),
            pltpu.VMEM((n_exp, rows, width), BF16),
            pltpu.VMEM((n_exp, rows, ff), BF16),
            pltpu.VMEM((n_exp, rows, ff), BF16),
            pltpu.VMEM((n_exp, rows, ff), BF16),
            pltpu.VMEM((chips, 2, n_exp * cap, width), BF16),
            pltpu.VMEM((chips, n_exp * cap, width), BF16),
            pltpu.VMEM((tok, width), F32),
            pltpu.VMEM((NZ, NR, half, width), F32),
            pltpu.VMEM((NZ, NR, half, width), F32),
            pltpu.VMEM((NZ, NR, half, width), F32),
            pltpu.VMEM((NZ + 2, NR, half, width), F32),
            dma((5,)), dma((4, chips)),
            dma((homes, 4)), dma((homes,)), dma((homes, 4)), dma((homes,)),
            dma((chips,)), dma((chips,)),
            dma((NZ, NR)), dma((NZ, NR)), dma((NZ, NR)), dma((NZ + 2, NR)),
        ],
        compiler_params=pltpu.CompilerParams(
            collective_id=0, has_side_effects=True, vmem_limit_bytes=62 * 2 ** 20),
    )(dy, meta, h1, h3, wg, wu, wd)


def weight_kernel(x_ref, dyd_ref, act_ref, dh1_ref, dh3_ref, gate_ref, up_ref, down_ref):
    def dot_0(a, b):
        return lax.dot_general(a, b, (((0,), (0,)), ((), ())), preferred_element_type=F32)

    gate_ref[0] = dot_0(x_ref[0], dh1_ref[0])
    up_ref[0] = dot_0(x_ref[0], dh3_ref[0])
    down_ref[0] = dot_0(act_ref[0], dyd_ref[0])


def weight_grads(x, dyd, act, dh1, dh3):
    n_exp, rows, width = x.shape
    ff = act.shape[2]
    tile = 256
    wide = pl.BlockSpec((1, rows, tile), lambda e, i: (e, 0, i))
    full = pl.BlockSpec((1, rows, ff), lambda e, i: (e, 0, 0))
    return pl.pallas_call(
        weight_kernel,
        grid=(n_exp, width // tile),
        in_specs=[wide, wide, full, full, full],
        out_specs=(pl.BlockSpec((1, tile, ff), lambda e, i: (e, i, 0)),
                   pl.BlockSpec((1, tile, ff), lambda e, i: (e, i, 0)),
                   pl.BlockSpec((1, ff, tile), lambda e, i: (e, 0, i))),
        out_shape=(jax.ShapeDtypeStruct((n_exp, width, ff), F32),
                   jax.ShapeDtypeStruct((n_exp, width, ff), F32),
                   jax.ShapeDtypeStruct((n_exp, ff, width), F32)),
        compiler_params=pltpu.CompilerParams(
            dimension_semantics=('arbitrary', 'arbitrary'), vmem_limit_bytes=60 * 2 ** 20),
    )(x, dyd, act, dh1, dh3)


def solution(mesh):
    ep_size = mesh.shape['ep']
    tok_spec = P(('dp', 'ep'), None)
    buf_spec = P(('dp', 'ep'), None, None)
    expert_spec = P('ep', None, None)

    def device_step(dy_loc, topk_idx, slot_idx, gates, y_back, x_disp, h1_disp, h3_disp, w_gate, w_up, w_down):
        cap = x_disp.shape[1] // ep_size
        top = topk_idx.shape[1]
        d_gates = jnp.einsum('td,tjd->tj', dy_loc, y_back, preferred_element_type=F32)
        flat = jnp.where(slot_idx >= 0, topk_idx * cap + slot_idx, -1).astype(F32)
        meta = jnp.concatenate([flat.T, gates.T], axis=0)
        dx_loc, dyd, act, dh1, dh3 = exchange(dy_loc, meta, h1_disp, h3_disp, w_gate, w_up, w_down, cap, top)
        dw_gate, dw_up, dw_down = weight_grads(x_disp, dyd, act, dh1, dh3)
        return dx_loc, d_gates, dw_gate, dw_up, dw_down

    return jax.shard_map(
        device_step, mesh=mesh,
        in_specs=(tok_spec, tok_spec, tok_spec, tok_spec, buf_spec, buf_spec, buf_spec, buf_spec,
                  expert_spec, expert_spec, expert_spec),
        out_specs=(tok_spec, tok_spec, buf_spec, buf_spec, buf_spec),
        check_vma=False)
```

time: 268 us -> 127 us (0.47)
  the two profiles are of different devices: /device:TPU:13 before, /device:TPU:14 now
where the time goes in v1:
time: 127 us
  Pallas kernels  121 us (95%)
  other arithmetic  1.99 us (2%)
  local copies, waits for them, and re-layouts  1.39 us (1%)
  matrix products  1.37 us (1%)
    pallas_call x1, Pallas kernels, exchange(): pl.pallas_call(functools.partial(exchange_kernel, tok, cap, top), out_sha...  107 us
    pallas_call x1, Pallas kernels, weight_grads(): pl.pallas_call(weight_kernel, grid=(n_exp, width // tile), in_specs=[wide...  14.5 us

profile of v1, /device:TPU:14, one launch (start us, length us, event | category | flops | bytes accessed | tf_op | source)
XLA Modules:
  0.0 126.7 jit_solution(14257931875347393095)
XLA Ops:
  0.6 0.7 convert_bitcast_fusion
  1.3 1.3 %pad_maximum_fusion.meta_ref = f32[16,128]{1,0:T(8,128)} fusion(f32[8,128]{1,0:T(8,128)} %bitcast.8, f32[8,128]{1,0:T(8,128)S(1)} %convert_bitcast_fusion), kind=kLoop, calls=%fused_computation.2 | loop fusion | flops 2048 | bytes 16384 | tf_op jit(solution)/shard_map/concatenate | solution.py:381
  2.6 106.8 %shard_map.146 = (bf16[128,1024]{1,0:T(8,128)(2,1)}, bf16[2,1024,1024]{2,1,0:T(8,128)(2,1)}, bf16[2,1024,512]{2,1,0:T(8,128)(2,1)}, bf16[2,1024,512]{2,1,0:T(8,128)(2,1)}, bf16[2,1024,512]{2,1,0:T(8,128)(2,1)}) custom-call(bf16[128,1024]{1,0:T(8,128)(2,1)} %dy_ref.1, f32[16,128]{1,0:T(8,128)} %pad_maximum_fusion.meta_ref, bf16[2,1024,512]{2,1,0:T(8,128)(2,1)} %h1_hbm.1, ...), custom_call_target="tpu_custom_call" | custom-call | tf_op jit(solution)/shard_map/pallas_call | solution.py:302
  109.4 0.0 copy-start
  109.5 0.0 copy-start.2
  109.5 14.5 %shard_map.147 = (f32[2,1024,512]{2,1,0:T(8,128)}, f32[2,1024,512]{2,1,0:T(8,128)}, f32[2,512,1024]{2,1,0:T(8,128)}) custom-call(bf16[2,1024,1024]{2,1,0:T(8,128)(2,1)} %x_ref.1, bf16[2,1024,1024]{2,1,0:T(8,128)(2,1)} %get-tuple-element.14.dyd_ref, bf16[2,1024,512]{2,1,0:T(8,128)(2,1)} %get-tuple-element.15.act_ref, ...), custom_call_target="tpu_custom_call" | custom-call | tf_op jit(solution)/shard_map/pallas_call | solution.py:355
  124.0 0.0 copy-done
  124.0 0.0 copy-done.2
  124.0 0.0 copy-start.1
  124.0 1.4 %fusion = f32[128,1,8]{2,1,0:T(1,128)S(1)} fusion(bf16[128,8,1024]{2,1,0:T(8,128)(2,1)S(1)} %copy-done.2, bf16[128,1024,1]{1,0,2:T(8,128)(2,1)S(1)} %bitcast.6), kind=kOutput, calls=%fused_computation | convolution fusion | flops 2097152 | bytes 2363392 | tf_op jit(solution)/shard_map/td,tjd->tj/dot_general | solution.py:379
  125.3 0.7 copy.17
  126.0 0.0 copy-done.1
  126.0 0.7 copy.21
Async XLA Ops:
  109.4 14.5 %copy-start = (bf16[128,1024]{1,0:T(8,128)(2,1)S(1)}, bf16[128,1024]{1,0:T(8,128)(2,1)}, u32[]{:S(2)}) copy-start(bf16[128,1024]{1,0:T(8,128)(2,1)} %dy_ref.1) | copy-start | bytes 786436
  109.5 14.5 %copy-start.2 = (bf16[128,8,1024]{2,1,0:T(8,128)(2,1)S(1)}, bf16[128,8,1024]{2,1,0:T(8,128)(2,1)}, u32[]{:S(2)}) copy-start(bf16[128,8,1024]{2,1,0:T(8,128)(2,1)} %param.15) | copy-start | bytes 6291460
  124.0 2.1 %copy-start.1 = (bf16[128,1024]{1,0:T(8,128)(2,1)S(1)}, bf16[128,1024]{1,0:T(8,128)(2,1)}, u32[]{:S(2)}) copy-start(bf16[128,1024]{1,0:T(8,128)(2,1)} %get-tuple-element.26) | copy-start | bytes 786436

commit v2 on v1

--- a/solution.py
+++ b/solution.py
@@ -11,7 +11,7 @@
 F32 = jnp.float32
 BF16 = jnp.bfloat16
 NZ = 4
-NR = 2
+NR = 4
 
 
 def line_pos(z, k):
@@ -23,15 +23,15 @@
     return q + 3 * far - 2 * far * q
 
 
-def dot_t(a, b):
-    return lax.dot_general(a, b, (((1,), (1,)), ((), ())), preferred_element_type=F32)
+def dot(a, b):
+    return jnp.dot(a, b, preferred_element_type=F32)
 
 
 def exchange_kernel(tok, cap, top,
                     dy_ref, meta_ref, h1_hbm, h3_hbm, wg_hbm, wu_hbm, wd_hbm,
                     dx_ref, dyd_hbm, act_hbm, dh1_hbm, dh3_hbm,
-                    gat, met, h1, h3, wg, wu, wd, dyd, act, dh1, dh3, xd, xr,
-                    own, sy, ry, sz, rz,
+                    gat, met, h1, h3, wg, wu, wd, wg_t, wu_t, wd_t, dyd, act, dh1, dh3, xd, xr,
+                    sp, ry, rz,
                     load_sem, out_sem, ag_send, ag_recv, mt_send, mt_recv,
                     xs_sem, xr_sem, sy_sem, ry_sem, sz_sem, rz_sem):
     me = lax.axis_index('ep')
@@ -91,30 +91,31 @@
     gat[me] = dy_ref[...]
     met[me] = meta_ref[...]
 
-    def from_line(k):
-        p = line_pos(z, k)
-        hid = home(p, y, c)
+    def arrive(p, yy):
+        hid = home(p, yy, c)
         ag_wait(hid)
         blk, mblk = gat.at[hid], met.at[hid]
 
-        @pl.when((p < z) & (z < NZ - 1))
+        @pl.when((p <= z) & (z < NZ - 1))
         def _():
             start(ag_copies(blk, mblk, hid, 2, dev(z + 1, y, c)))
 
-        @pl.when((p > z) & (z > 0))
+        @pl.when((p >= z) & (z > 0))
         def _():
             start(ag_copies(blk, mblk, hid, 3, dev(z - 1, y, c)))
 
-        start(ag_copies(blk, mblk, hid, 1, dev(z, oy, c)))
         start(ag_copies(blk, mblk, hid, 0, dev(z, y, oc)))
-
-    def from_pair(k):
-        hid = home(line_pos(z, k), oy, c)
-        ag_wait(hid)
-        start(ag_copies(gat.at[hid], met.at[hid], hid, 0, dev(z, y, oc)))
 
     for cp in loads:
         cp.wait()
+
+    def turn(e, carry):
+        wd_t[e] = wd[e].T
+        wg_t[e] = wg[e].T
+        wu_t[e] = wu[e].T
+        return carry
+
+    lax.fori_loop(0, 2, turn, 0)
 
     def xs_copy(chip):
         return pltpu.make_async_remote_copy(xd.at[chip, oc], xr.at[chip], xs_sem.at[chip], xr_sem.at[chip],
@@ -146,12 +147,12 @@
         pick = jnp.concatenate(picks, axis=0).astype(BF16)
         gate = jnp.concatenate(row_gate, axis=0)
         pair = jnp.concatenate([gat[chip * 2], gat[chip * 2 + 1]], axis=0)
-        picked = jnp.dot(pick, pair, preferred_element_type=F32)
+        picked = dot(pick, pair)
         rows_dy = (picked * gate).astype(BF16)
         for e in range(2):
             dy_e = rows_dy[e * 2 * cap:(e + 1) * 2 * cap]
             dyd[e, rows] = dy_e
-            d_act = dot_t(dy_e, wd[e]).astype(BF16).astype(F32)
+            d_act = dot(dy_e, wd_t[e]).astype(BF16).astype(F32)
             gate_f = h1[e, rows].astype(F32)
             up_f = h3[e, rows].astype(F32)
             sig = jax.nn.sigmoid(gate_f)
@@ -161,32 +162,12 @@
             d3 = (d_act * silu).astype(BF16)
             dh1[e, rows] = d1
             dh3[e, rows] = d3
-            d_x = (dot_t(d1, wg[e]) + dot_t(d3, wu[e])).astype(BF16)
+            d_x = (dot(d1, wg_t[e]) + dot(d3, wu_t[e])).astype(BF16)
             for h in range(2):
                 xd[chip, h, e * cap:(e + 1) * cap] = d_x[h * cap:(h + 1) * cap]
         xs_copy(chip).start()
         for cp in out_copies(chip):
             cp.start()
-
-    def step(n, carry):
-        k, side = n // 2, n % 2
-
-        @pl.when((side == 0) & (k < NZ - 1))
-        def _():
-            from_line(k + 1)
-            from_pair(k)
-
-        @pl.when((side == 1) & (k == NZ - 1))
-        def _():
-            from_pair(k)
-
-        yy = y + side - 2 * y * side
-        p = line_pos(z, k)
-        ag_wait(home(p, yy, oc))
-        group(p * 2 + yy)
-        return carry
-
-    lax.fori_loop(0, 2 * NZ, step, 0)
 
     row_id = lax.broadcasted_iota(jnp.int32, (2 * cap, 1), 0).astype(F32)
 
@@ -201,80 +182,144 @@
         vals = jnp.concatenate([xd[chip, c], xr[chip]], axis=0)
         return lax.dot_general(hit.astype(BF16), vals, (((0,), (0,)), ((), ())), preferred_element_type=F32)
 
-    half = tok // NR
+    chunk = tok // NR
+
+    def keep(side, k, chip):
+        part = partial(chip)
+        for i in range(NR):
+            sp[side, k, i] = part[i * chunk:(i + 1) * chunk]
 
     def y_copy(k, i):
-        return pltpu.make_async_remote_copy(sy.at[k, i], ry.at[k, i], sy_sem.at[k, i], ry_sem.at[k, i],
+        return pltpu.make_async_remote_copy(sp.at[1, k, i], ry.at[k, i], sy_sem.at[k, i], ry_sem.at[k, i],
                                             device_id=dev(z, oy, c), device_id_type=MESH)
 
     def z_copy(k, i, target_z, to_slot):
-        return pltpu.make_async_remote_copy(sz.at[k, i], rz.at[to_slot, i], sz_sem.at[k, i], rz_sem.at[to_slot, i],
+        return pltpu.make_async_remote_copy(sp.at[0, k, i], rz.at[to_slot, i], sz_sem.at[k, i], rz_sem.at[to_slot, i],
                                             device_id=dev(target_z, y, c), device_id_type=MESH)
 
     def z_wait(from_slot, i):
         z_copy(0, i, z, from_slot).wait_recv()
 
-    for k in (3, 2, 1, 0):
-        part = partial(line_pos(z, k) * 2 + oy)
-        for i in range(NR):
-            sy[k, i] = part[i * half:(i + 1) * half]
-            y_copy(k, i).start()
-
-    for k in (3, 1, 2):
+    inner = z * (NZ - 1 - z) // 2
+    at_end = inner == 0
+    inside = inner == 1
+
+    def pass_on(k, i):
         p = line_pos(z, k)
         way = jnp.where(p > z, 1, -1)
-        own[...] = partial(p * 2 + y)
         behind = z - way
-        has_in = (behind >= 0) & (behind < NZ)
         ahead = z + way
         to_slot = jnp.where(ahead == p, jnp.where(way > 0, NZ, NZ + 1), p)
+        y_copy(k, i).wait_recv()
+        sp[0, k, i] += ry[k, i]
+
+        @pl.when((behind >= 0) & (behind < NZ))
+        def _():
+            z_wait(p, i)
+            sp[0, k, i] += rz[p, i]
+
+        z_copy(k, i, ahead, to_slot).start()
+
+    def step(n, carry):
+        is3 = (n + 5) // 8 - (n + 4) // 8
+        is4 = (n + 4) // 8 - (n + 3) // 8
+        k = n // 2 + inner * (is3 - is4)
+        side = n % 2 - inner * (is3 - is4)
+        yy = y + side - 2 * y * side
+        p = line_pos(z, k)
+
+        @pl.when(n > 0)
+        def _():
+            arrive(p, yy)
+
+        ag_wait(home(p, yy, oc))
+        group(p * 2 + yy)
+
+        @pl.when(side == 1)
+        def _():
+            keep(0, k, p * 2 + y)
+            keep(1, k, p * 2 + oy)
+            for i in range(NR // 2):
+                y_copy(k, i).start()
+
+            @pl.when(k > 0)
+            def _():
+                for i in range(NR // 2, NR):
+                    y_copy(k, i).start()
+
+            @pl.when(k == NZ - 1)
+            def _():
+                for i in range(NR // 2, NR):
+                    y_copy(0, i).start()
+
+        @pl.when((n == 4) & at_end)
+        def _():
+            pass_on(1, 0)
+
+        @pl.when((n == 5) & at_end)
+        def _():
+            pass_on(1, 1)
+            pass_on(1, 2)
+
+        @pl.when((n == 6) & at_end)
+        def _():
+            pass_on(1, 3)
+            pass_on(2, 0)
+            pass_on(2, 1)
+
+        return carry
+
+    lax.fori_loop(0, 2 * NZ, step, 0)
+
+    @pl.when(at_end)
+    def _():
+        pass_on(2, 2)
+        pass_on(2, 3)
         for i in range(NR):
-            y_copy(k, i).wait_recv()
-            sz[k, i] = own[i * half:(i + 1) * half] + ry[k, i]
-
-            @pl.when(has_in)
-            def _():
-                z_wait(p, i)
-                sz[k, i] += rz[p, i]
-
-            z_copy(k, i, ahead, to_slot).start()
-
-    own[...] = partial(z * 2 + y)
+            pass_on(3, i)
+
+    @pl.when(inside)
+    def _():
+        for i in range(NR):
+            pass_on(2, i)
+        for i in range(NR):
+            pass_on(3, i)
+            pass_on(1, i)
+
     for i in range(NR):
-        rows = slice(i * half, (i + 1) * half)
         y_copy(0, i).wait_recv()
-        own[rows] += ry[0, i]
+        sp[0, 0, i] += ry[0, i]
 
         @pl.when(z > 0)
         def _():
             z_wait(NZ, i)
-            own[rows] += rz[NZ, i]
+            sp[0, 0, i] += rz[NZ, i]
 
         @pl.when(z < NZ - 1)
         def _():
             z_wait(NZ + 1, i)
-            own[rows] += rz[NZ + 1, i]
-
-        dx_ref[rows] = own[rows].astype(BF16)
+            sp[0, 0, i] += rz[NZ + 1, i]
+
+        dx_ref[i * chunk:(i + 1) * chunk] = sp[0, 0, i].astype(BF16)
 
     def ag_sent(hid, way):
         for cp in ag_copies(gat.at[hid], met.at[hid], hid, way, dev(z, y, oc)):
             cp.wait_send()
 
+    ag_sent(me, 1)
     for k in range(NZ):
         p = line_pos(z, k)
-        hid = home(p, y, c)
-        ag_sent(hid, 0)
-        ag_sent(hid, 1)
-        ag_sent(home(p, oy, c), 0)
-
-        @pl.when((p <= z) & (z < NZ - 1))
-        def _():
-            ag_sent(hid, 2)
-
-        @pl.when((p >= z) & (z > 0))
-        def _():
-            ag_sent(hid, 3)
+        for yy in range(2):
+            hid = home(p, yy, c)
+            ag_sent(hid, 0)
+
+            @pl.when((p <= z) & (z < NZ - 1))
+            def _():
+                ag_sent(hid, 2)
+
+            @pl.when((p >= z) & (z > 0))
+            def _():
+                ag_sent(hid, 3)
 
         for i in range(NR):
             y_copy(k, i).wait_send()
@@ -295,7 +340,7 @@
     n_exp, rows, ff = h1.shape
     homes = rows // cap
     chips = homes // 2
-    half = tok // NR
+    chunk = tok // NR
     dma = pltpu.SemaphoreType.DMA
     any_spec = pl.BlockSpec(memory_space=pl.ANY)
     vmem_spec = pl.BlockSpec(memory_space=pltpu.VMEM)
@@ -316,17 +361,18 @@
             pltpu.VMEM(wg.shape, BF16),
             pltpu.VMEM(wu.shape, BF16),
             pltpu.VMEM(wd.shape, BF16),
+            pltpu.VMEM((n_exp, ff, width), BF16),
+            pltpu.VMEM((n_exp, ff, width), BF16),
+            pltpu.VMEM((n_exp, width, ff), BF16),
             pltpu.VMEM((n_exp, rows, width), BF16),
             pltpu.VMEM((n_exp, rows, ff), BF16),
             pltpu.VMEM((n_exp, rows, ff), BF16),
             pltpu.VMEM((n_exp, rows, ff), BF16),
             pltpu.VMEM((chips, 2, n_exp * cap, width), BF16),
             pltpu.VMEM((chips, n_exp * cap, width), BF16),
-            pltpu.VMEM((tok, width), F32),
-            pltpu.VMEM((NZ, NR, half, width), F32),
-            pltpu.VMEM((NZ, NR, half, width), F32),
-            pltpu.VMEM((NZ, NR, half, width), F32),
-            pltpu.VMEM((NZ + 2, NR, half, width), F32),
+            pltpu.VMEM((2, NZ, NR, chunk, width), F32),
+            pltpu.VMEM((NZ, NR, chunk, width), F32),
+            pltpu.VMEM((NZ + 2, NR, chunk, width), F32),
             dma((5,)), dma((4, chips)),
             dma((homes, 4)), dma((homes,)), dma((homes, 4)), dma((homes,)),
             dma((chips,)), dma((chips,)),

time: 127 us -> 109 us (0.86)
  the two profiles are of different devices: /device:TPU:14 before, /device:TPU:0 now
where the time goes in v2:
time: 109 us
  Pallas kernels  104 us (95%)
  other arithmetic  1.99 us (2%)
  local copies, waits for them, and re-layouts  1.39 us (1%)
  matrix products  1.37 us (1%)
    pallas_call x1, Pallas kernels, exchange(): pl.pallas_call(functools.partial(exchange_kernel, tok, cap, top), out_sha...  89 us
    pallas_call x1, Pallas kernels, weight_grads(): pl.pallas_call(weight_kernel, grid=(n_exp, width // tile), in_specs=[wide...  14.5 us

profile of v2, /device:TPU:0, one launch (start us, length us, event | category | flops | bytes accessed | tf_op | source)
XLA Modules:
  0.0 108.9 jit_solution(10835817152840076519)
XLA Ops:
  0.6 0.7 convert_bitcast_fusion
  1.3 1.3 %pad_maximum_fusion.meta_ref = f32[16,128]{1,0:T(8,128)} fusion(f32[8,128]{1,0:T(8,128)} %bitcast.8, f32[8,128]{1,0:T(8,128)S(1)} %convert_bitcast_fusion), kind=kLoop, calls=%fused_computation.2 | loop fusion | flops 2048 | bytes 16384 | tf_op jit(solution)/shard_map/concatenate | solution.py:427
  2.6 89.0 %shard_map.146 = (bf16[128,1024]{1,0:T(8,128)(2,1)}, bf16[2,1024,1024]{2,1,0:T(8,128)(2,1)}, bf16[2,1024,512]{2,1,0:T(8,128)(2,1)}, bf16[2,1024,512]{2,1,0:T(8,128)(2,1)}, bf16[2,1024,512]{2,1,0:T(8,128)(2,1)}) custom-call(bf16[128,1024]{1,0:T(8,128)(2,1)} %dy_ref.1, f32[16,128]{1,0:T(8,128)} %pad_maximum_fusion.meta_ref, bf16[2,1024,512]{2,1,0:T(8,128)(2,1)} %h1_hbm.1, ...), custom_call_target="tpu_custom_call" | custom-call | tf_op jit(solution)/shard_map/pallas_call | solution.py:347
  91.7 0.0 copy-start
  91.7 0.0 copy-start.2
  91.7 14.5 %shard_map.147 = (f32[2,1024,512]{2,1,0:T(8,128)}, f32[2,1024,512]{2,1,0:T(8,128)}, f32[2,512,1024]{2,1,0:T(8,128)}) custom-call(bf16[2,1024,1024]{2,1,0:T(8,128)(2,1)} %x_ref.1, bf16[2,1024,1024]{2,1,0:T(8,128)(2,1)} %get-tuple-element.14.dyd_ref, bf16[2,1024,512]{2,1,0:T(8,128)(2,1)} %get-tuple-element.15.act_ref, ...), custom_call_target="tpu_custom_call" | custom-call | tf_op jit(solution)/shard_map/pallas_call | solution.py:401
  106.2 0.0 copy-done
  106.2 0.0 copy-done.2
  106.2 0.0 copy-start.1
  106.2 1.4 %fusion = f32[128,1,8]{2,1,0:T(1,128)S(1)} fusion(bf16[128,8,1024]{2,1,0:T(8,128)(2,1)S(1)} %copy-done.2, bf16[128,1024,1]{1,0,2:T(8,128)(2,1)S(1)} %bitcast.6), kind=kOutput, calls=%fused_computation | convolution fusion | flops 2097152 | bytes 2363392 | tf_op jit(solution)/shard_map/td,tjd->tj/dot_general | solution.py:425
  107.6 0.7 copy.17
  108.2 0.0 copy-done.1
  108.2 0.7 copy.21
Async XLA Ops:
  91.7 14.5 %copy-start = (bf16[128,1024]{1,0:T(8,128)(2,1)S(1)}, bf16[128,1024]{1,0:T(8,128)(2,1)}, u32[]{:S(2)}) copy-start(bf16[128,1024]{1,0:T(8,128)(2,1)} %dy_ref.1) | copy-start | bytes 786436
  91.7 14.5 %copy-start.2 = (bf16[128,8,1024]{2,1,0:T(8,128)(2,1)S(1)}, bf16[128,8,1024]{2,1,0:T(8,128)(2,1)}, u32[]{:S(2)}) copy-start(bf16[128,8,1024]{2,1,0:T(8,128)(2,1)} %param.15) | copy-start | bytes 6291460
  106.2 2.1 %copy-start.1 = (bf16[128,1024]{1,0:T(8,128)(2,1)S(1)}, bf16[128,1024]{1,0:T(8,128)(2,1)}, u32[]{:S(2)}) copy-start(bf16[128,1024]{1,0:T(8,128)(2,1)} %get-tuple-element.26) | copy-start | bytes 786436

commit v3 on v2

v3 whole, which is shorter than its diff:
```python
import functools

import jax
import jax.numpy as jnp
from jax import lax
from jax.experimental import pallas as pl
from jax.experimental.pallas import tpu as pltpu
from jax.sharding import PartitionSpec as P

MESH = pl.DeviceIdType.MESH
F32 = jnp.float32
BF16 = jnp.bfloat16
NZ = 4
NR = 4


def line_pos(z, k):
    edge = z * (3 - z) // 2
    far = z // 2
    is0 = (3 - k) // 3
    is1 = (k + 2) // 3 - (k + 1) // 3
    q = k + edge * is0 - edge * is1
    return q + 3 * far - 2 * far * q


def dot(a, b):
    return jnp.dot(a, b, preferred_element_type=F32)


def exchange_kernel(tok, cap, top,
                    dy_ref, topk_ref, slot_ref, gates_ref, yb_hbm, x_hbm, h1_hbm, h3_hbm, wg_hbm, wu_hbm, wd_hbm,
                    dx_ref, dgate_ref, dwg_ref, dwu_ref, dwd_ref,
                    gat, met, mine, h1, h3, wg_t, wu_t, wd_t, xb, yb, dyd, act, xd, xr, sp, ry, rz, lanes,
                    load_sem, ag_send, ag_recv, mt_send, mt_recv,
                    xs_sem, xr_sem, sy_sem, ry_sem, sz_sem, rz_sem):
    me = lax.axis_index('ep')
    dp = lax.axis_index('dp')
    z, y, c = me // 4, (me // 2) % 2, me % 2
    oy, oc = 1 - y, 1 - c

    def dev(z_, y_, c_):
        return (dp, (z_ * 2 + y_) * 2 + c_)

    def home(z_, y_, c_):
        return (z_ * 2 + y_) * 2 + c_

    ff = h1.shape[2]
    raw_d, raw_g, raw_u = dyd.at[:, 0:ff, :], xb.at[:, :, 0:ff], xb.at[:, :, ff:2 * ff]
    loads = [pltpu.make_async_copy(s, d, load_sem.at[i]) for i, (s, d) in enumerate(
        ((wd_hbm, raw_d), (wg_hbm, raw_g), (wu_hbm, raw_u), (h1_hbm, h1), (h3_hbm, h3), (yb_hbm, yb)))]
    for cp in loads:
        cp.start()
    x_load = pltpu.make_async_copy(x_hbm, xb, load_sem.at[6])

    mine[0:top] = jnp.where(slot_ref[...] >= 0, topk_ref[...] * cap + slot_ref[...], -1).astype(F32)
    mine[top:2 * top] = gates_ref[...]

    barrier = pltpu.get_barrier_semaphore()
    pl.semaphore_signal(barrier, inc=1, device_id=dev(z, y, oc), device_id_type=MESH)
    pl.semaphore_signal(barrier, inc=1, device_id=dev(z, oy, c), device_id_type=MESH)

    @pl.when(z > 0)
    def _():
        pl.semaphore_signal(barrier, inc=1, device_id=dev(z - 1, y, c), device_id_type=MESH)

    @pl.when(z < NZ - 1)
    def _():
        pl.semaphore_signal(barrier, inc=1, device_id=dev(z + 1, y, c), device_id_type=MESH)

    @pl.when((z == 0) | (z == NZ - 1))
    def _():
        pl.semaphore_signal(barrier, inc=1, device_id=dev(NZ - 1 - z, y, c), device_id_type=MESH)

    pl.semaphore_wait(barrier, 4)

    def ag_copies(src, msrc, hid, way, target):
        return (pltpu.make_async_remote_copy(src, gat.at[hid], ag_send.at[hid, way], ag_recv.at[hid],
                                             device_id=target, device_id_type=MESH),
                pltpu.make_async_remote_copy(msrc, met.at[hid], mt_send.at[hid, way], mt_recv.at[hid],
                                             device_id=target, device_id_type=MESH))

    def start(copies):
        for cp in copies:
            cp.start()

    def ag_wait(hid):
        for cp in ag_copies(gat.at[hid], met.at[hid], hid, 0, dev(z, y, oc)):
            cp.wait_recv()

    @pl.when(z < NZ - 1)
    def _():
        start(ag_copies(dy_ref, mine, me, 2, dev(z + 1, y, c)))

    @pl.when(z > 0)
    def _():
        start(ag_copies(dy_ref, mine, me, 3, dev(z - 1, y, c)))

    start(ag_copies(dy_ref, mine, me, 1, dev(z, oy, c)))
    start(ag_copies(dy_ref, mine, me, 0, dev(z, y, oc)))
    gat[me] = dy_ref[...]
    met[me] = mine[...]

    def arrive(p, yy):
        hid = home(p, yy, c)
        ag_wait(hid)
        blk, mblk = gat.at[hid], met.at[hid]

        @pl.when((p <= z) & (z < NZ - 1))
        def _():
            start(ag_copies(blk, mblk, hid, 2, dev(z + 1, y, c)))

        @pl.when((p >= z) & (z > 0))
        def _():
            start(ag_copies(blk, mblk, hid, 3, dev(z - 1, y, c)))

        start(ag_copies(blk, mblk, hid, 0, dev(z, y, oc)))

    def turn(e, carry):
        wd_t[e] = dyd[e, 0:ff, :].T
        wg_t[e] = xb[e, :, 0:ff].T
        wu_t[e] = xb[e, :, ff:2 * ff].T
        return carry

    with jax.named_scope('turn'):
        for cp in loads:
            cp.wait()
        lax.fori_loop(0, 2, turn, 0)
        x_load.start()

    def xs_copy(chip):
        return pltpu.make_async_remote_copy(xd.at[chip, oc], xr.at[chip], xs_sem.at[chip], xr_sem.at[chip],
                                            device_id=dev(z, y, oc), device_id_type=MESH)

    slot = lax.broadcasted_iota(jnp.int32, (cap, 1), 0).astype(F32)

    def group(chip):
        first = (me * 2 * cap).astype(F32)
        rows = pl.ds(chip * 2 * cap, 2 * cap)
        picks, row_gate = [], []
        for e in range(2):
            for h in range(2):
                want = slot + (first + float(e * cap))
                hit = jnp.zeros((cap, tok), F32)
                gsum = jnp.zeros((cap, tok), F32)
                for j in range(top):
                    same = met[chip * 2 + h, j:j + 1, :] == want
                    hit = jnp.where(same, 1.0, hit)
                    gsum = jnp.where(same, met[chip * 2 + h, top + j:top + j + 1, :], gsum)
                row_gate.append(jnp.sum(gsum, axis=1, keepdims=True))
                none = jnp.zeros((cap, tok), F32)
                picks.append(jnp.concatenate([hit, none] if h == 0 else [none, hit], axis=1))
        pick = jnp.concatenate(picks, axis=0).astype(BF16)
        gate = jnp.concatenate(row_gate, axis=0)
        pair = jnp.concatenate([gat[chip * 2], gat[chip * 2 + 1]], axis=0)
        picked = dot(pick, pair)
        rows_dy = (picked * gate).astype(BF16)
        for e in range(2):
            dy_e = rows_dy[e * 2 * cap:(e + 1) * 2 * cap]
            dyd[e, rows] = dy_e
            d_act = dot(dy_e, wd_t[e]).astype(BF16).astype(F32)
            gate_f = h1[e, rows].astype(F32)
            up_f = h3[e, rows].astype(F32)
            sig = jax.nn.sigmoid(gate_f)
            silu = gate_f * sig
            act[e, rows] = (silu * up_f).astype(BF16)
            d1 = (d_act * up_f * sig * (1.0 + gate_f * (1.0 - sig))).astype(BF16)
            d3 = (d_act * silu).astype(BF16)
            h1[e, rows] = d1
            h3[e, rows] = d3
            d_x = (dot(d1, wg_t[e]) + dot(d3, wu_t[e])).astype(BF16)
            for h in range(2):
                xd[chip, h, e * cap:(e + 1) * cap] = d_x[h * cap:(h + 1) * cap]
        xs_copy(chip).start()

    row_id = lax.broadcasted_iota(jnp.int32, (2 * cap, 1), 0).astype(F32)

    def partial(chip):
        hid = chip * 2 + c
        xs_copy(chip).wait_recv()
        want = jnp.concatenate([row_id + (me * 2 * cap).astype(F32),
                                row_id + ((me + 1 - 2 * c) * 2 * cap).astype(F32)], axis=0)
        hit = jnp.zeros((4 * cap, tok), F32)
        for j in range(top):
            hit = jnp.where(met[hid, j:j + 1, :] == want, 1.0, hit)
        vals = jnp.concatenate([xd[chip, c], xr[chip]], axis=0)
        return lax.dot_general(hit.astype(BF16), vals, (((0,), (0,)), ((), ())), preferred_element_type=F32)

    chunk = tok // NR

    def keep(side, k, chip):
        part = partial(chip)
        for i in range(NR):
            sp[side, k, i] = part[i * chunk:(i + 1) * chunk]

    def y_copy(k, i):
        return pltpu.make_async_remote_copy(sp.at[1, k, i], ry.at[k, i], sy_sem.at[k, i], ry_sem.at[k, i],
                                            device_id=dev(z, oy, c), device_id_type=MESH)

    def z_copy(k, i, target_z, to_slot):
        return pltpu.make_async_remote_copy(sp.at[0, k, i], rz.at[to_slot, i], sz_sem.at[k, i], rz_sem.at[to_slot, i],
                                            device_id=dev(target_z, y, c), device_id_type=MESH)

    def z_wait(from_slot, i):
        z_copy(0, i, z, from_slot).wait_recv()

    inner = z * (NZ - 1 - z) // 2
    at_end = inner == 0
    inside = inner == 1

    def pass_on(k, i):
        p = line_pos(z, k)
        way = jnp.where(p > z, 1, -1)
        behind = z - way
        ahead = z + way
        across = at_end & (k == NZ - 1)
        to_slot = jnp.where(ahead == p, jnp.where(way > 0, NZ, NZ + 1), p)
        y_copy(k, i).wait_recv()
        sp[0, k, i] += ry[k, i]

        @pl.when((behind >= 0) & (behind < NZ) & (k < NZ - 1))
        def _():
            z_wait(p, i)
            sp[0, k, i] += rz[p, i]

        z_copy(k, i, jnp.where(across, p, ahead), jnp.where(across, NZ + 2, to_slot)).start()

    tile = 256
    per = (2 * ff) // tile

    def dot_0(a_, b_):
        return lax.dot_general(a_, b_, (((0,), (0,)), ((), ())), preferred_element_type=F32)

    def weight_unit(u):
        @pl.when(u < 2 * per)
        def _():
            e, m = u // per, u % per
            cols = pl.ds(pl.multiple_of(m * tile, tile), tile)
            part = xb[e, :, cols]
            dwg_ref[e, cols] = dot_0(part, h1[e])
            dwu_ref[e, cols] = dot_0(part, h3[e])

        @pl.when(u >= 2 * per)
        def _():
            v = u - 2 * per
            e, m = v // (per // 2), v % (per // 2)
            cols = pl.ds(pl.multiple_of(m * tile, tile), tile)
            dwd_ref[e, cols] = dot_0(act[e, :, cols], dyd[e])

    n_unit = 3 * per

    def gate_rows(i, carry):
        few = 8
        t0 = pl.multiple_of(i * few, few)
        d = dy_ref[pl.ds(t0, few)].astype(F32)
        prod = yb[pl.ds(t0, few)].astype(F32) * d[:, None, :]
        acc = prod[:, :, 0:128]
        for q in range(1, prod.shape[2] // 128):
            acc = acc + prod[:, :, q * 128:(q + 1) * 128]
        lanes[pl.ds(pl.multiple_of(t0 * top, few * top), few * top)] = acc.reshape(few * top, 128)
        return carry

    def gate_grads():
        lax.fori_loop(0, tok // 8, gate_rows, 0)
        for j in range(top):
            dgate_ref[j:j + 1] = jnp.sum(lanes[pl.ds(j, tok, stride=top)].T, axis=0, keepdims=True)

    def place(n, mid):
        is3 = (n + 5) // 8 - (n + 4) // 8
        is4 = (n + 4) // 8 - (n + 3) // 8
        k = n // 2 + mid * (is3 - is4)
        side = n % 2 - mid * (is3 - is4)
        return k, side

    def arrive_at(n, mid):
        k, side = place(n, mid)
        with jax.named_scope('arrive'):
            arrive(line_pos(z, k), y + side - 2 * y * side)

    def y_send(k, lo, hi):
        for i in range(lo, hi):
            y_copy(k, i).start()

    mid_arrivals = {1: (1, 2, 3), 4: (4, 5), 6: (6,), 7: (7,)}
    mid_keeps = {2: 0, 5: 1, 6: 2, 7: 3}
    half = NR // 2

    def step(n, carry):
        k, side = place(n, inner)
        p = line_pos(z, k)
        yy = y + side - 2 * y * side

        @pl.when(at_end & (n > 0))
        def _():
            arrive_at(n, 0)

        for n0, blocks in mid_arrivals.items():
            @pl.when(inside & (n == n0))
            def _():
                for m in blocks:
                    arrive_at(m, 1)

        @pl.when(at_end & (n == 7))
        def _():
            for i in range(half):
                pass_on(2, i)

        with jax.named_scope('other_core'):
            ag_wait(home(p, yy, oc))
        with jax.named_scope('group'):
            group(p * 2 + yy)

        mid_keep = (n == 2) | (n == 5) | (n == 6) | (n == 7)

        @pl.when((at_end & (side == 1)) | (inside & mid_keep))
        def _():
            kk = jnp.where(at_end, k, (n - 1) // 4 + n // 6 + n // 7)
            q = line_pos(z, kk)
            with jax.named_scope('keep'):
                keep(1, kk, q * 2 + oy)

                @pl.when(kk == 0)
                def _():
                    y_send(0, 0, half)

                @pl.when((kk == 1) | (kk == 3) | (at_end & (kk == 2)))
                def _():
                    y_send(kk, 0, NR)

                @pl.when(inside & (kk == 3))
                def _():
                    y_send(2, 0, NR)

                @pl.when(kk == 3)
                def _():
                    y_send(0, half, NR)

                keep(0, kk, q * 2 + y)

        @pl.when((n == 4) & at_end)
        def _():
            pass_on(1, 0)

        @pl.when((n == 5) & at_end)
        def _():
            for i in range(1, NR):
                pass_on(1, i)

        return carry

    lax.fori_loop(0, 2 * NZ, step, 0)

    x_load.wait()
    end_order = [(2, i) for i in range(half, NR)] + [(3, i) for i in range(NR)]
    mid_order = [(3, 0), (3, 1), (1, 0), (3, 2), (1, 1), (3, 3), (1, 2), (2, 0), (1, 3), (2, 1), (2, 2), (2, 3)]

    def late(m, carry):
        with jax.named_scope('weights'):
            weight_unit(m)

        with jax.named_scope('pass_on'):
            for m0, (k, i) in enumerate(end_order):
                @pl.when(at_end & (m == m0))
                def _():
                    pass_on(k, i)

            for m0, (k, i) in enumerate(mid_order):
                @pl.when(inside & (m == m0))
                def _():
                    pass_on(k, i)

        return carry

    lax.fori_loop(0, n_unit, late, 0)
    with jax.named_scope('gates'):
        gate_grads()

    for i in range(NR):
        with jax.named_scope('final'):
            y_copy(0, i).wait_recv()
        sp[0, 0, i] += ry[0, i]

        @pl.when(z > 0)
        def _():
            z_wait(NZ, i)
            sp[0, 0, i] += rz[NZ, i]

        @pl.when(z < NZ - 1)
        def _():
            z_wait(NZ + 1, i)
            sp[0, 0, i] += rz[NZ + 1, i]

        @pl.when(at_end)
        def _():
            z_wait(NZ + 2, i)
            sp[0, 0, i] += rz[NZ + 2, i]

        dx_ref[i * chunk:(i + 1) * chunk] = sp[0, 0, i].astype(BF16)

    def ag_sent(hid, way):
        for cp in ag_copies(gat.at[hid], met.at[hid], hid, way, dev(z, y, oc)):
            cp.wait_send()

    ag_sent(me, 1)
    for k in range(NZ):
        p = line_pos(z, k)
        for yy in range(2):
            hid = home(p, yy, c)
            ag_sent(hid, 0)

            @pl.when((p <= z) & (z < NZ - 1))
            def _():
                ag_sent(hid, 2)

            @pl.when((p >= z) & (z > 0))
            def _():
                ag_sent(hid, 3)

        for i in range(NR):
            y_copy(k, i).wait_send()
            if k:
                z_copy(k, i, z, 0).wait_send()

    def drain(chip, carry):
        xs_copy(chip).wait_send()
        return carry

    lax.fori_loop(0, 2 * NZ, drain, 0)


def exchange(dy, topk, slot, gates, yb, x, h1, h3, wg, wu, wd, cap):
    tok, width = dy.shape
    top = topk.shape[0]
    n_exp, rows, ff = h1.shape
    homes = rows // cap
    chips = homes // 2
    chunk = tok // NR
    dma = pltpu.SemaphoreType.DMA
    any_spec = pl.BlockSpec(memory_space=pl.ANY)
    vmem_spec = pl.BlockSpec(memory_space=pltpu.VMEM)
    return pl.pallas_call(
        functools.partial(exchange_kernel, tok, cap, top),
        out_shape=(pltpu.VMEM((tok, width), BF16),
                   pltpu.VMEM((top, tok), F32),
                   pltpu.VMEM((n_exp, width, ff), F32),
                   pltpu.VMEM((n_exp, width, ff), F32),
                   pltpu.VMEM((n_exp, ff, width), F32)),
        in_specs=[vmem_spec] * 4 + [any_spec] * 7,
        out_specs=(vmem_spec,) * 5,
        scratch_shapes=[
            pltpu.VMEM((homes, tok, width), BF16),
            pltpu.VMEM((homes, 2 * top, tok), F32),
            pltpu.VMEM((2 * top, tok), F32),
            pltpu.VMEM(h1.shape, BF16),
            pltpu.VMEM(h3.shape, BF16),
            pltpu.VMEM((n_exp, ff, width), BF16),
            pltpu.VMEM((n_exp, ff, width), BF16),
            pltpu.VMEM((n_exp, width, ff), BF16),
            pltpu.VMEM(x.shape, BF16),
            pltpu.VMEM(yb.shape, BF16),
            pltpu.VMEM((n_exp, rows, width), BF16),
            pltpu.VMEM((n_exp, rows, ff), BF16),
            pltpu.VMEM((chips, 2, n_exp * cap, width), BF16),
            pltpu.VMEM((chips, n_exp * cap, width), BF16),
            pltpu.VMEM((2, NZ, NR, chunk, width), F32),
            pltpu.VMEM((NZ, NR, chunk, width), F32),
            pltpu.VMEM((NZ + 3, NR, chunk, width), F32),
            pltpu.VMEM((tok * top, 128), F32),
            dma((7,)),
            dma((homes, 4)), dma((homes,)), dma((homes, 4)), dma((homes,)),
            dma((chips,)), dma((chips,)),
            dma((NZ, NR)), dma((NZ, NR)), dma((NZ, NR)), dma((NZ + 3, NR)),
        ],
        compiler_params=pltpu.CompilerParams(
            collective_id=0, has_side_effects=True, vmem_limit_bytes=48 * 2 ** 20),
    )(dy, topk, slot, gates, yb, x, h1, h3, wg, wu, wd)


def solution(mesh):
    ep_size = mesh.shape['ep']
    tok_spec = P(('dp', 'ep'), None)
    buf_spec = P(('dp', 'ep'), None, None)
    expert_spec = P('ep', None, None)

    def device_step(dy_loc, topk_idx, slot_idx, gates, y_back, x_disp, h1_disp, h3_disp, w_gate, w_up, w_down):
        cap = x_disp.shape[1] // ep_size
        dx_loc, d_gates, dw_gate, dw_up, dw_down = exchange(
            dy_loc, topk_idx.T, slot_idx.T, gates.T, y_back, x_disp, h1_disp, h3_disp,
            w_gate, w_up, w_down, cap)
        return dx_loc, d_gates.T, dw_gate, dw_up, dw_down

    return jax.shard_map(
        device_step, mesh=mesh,
        in_specs=(tok_spec, tok_spec, tok_spec, tok_spec, buf_spec, buf_spec, buf_spec, buf_spec,
                  expert_spec, expert_spec, expert_spec),
        out_specs=(tok_spec, tok_spec, buf_spec, buf_spec, buf_spec),
        check_vma=False)
```

time: 109 us -> 85.9 us (0.79)
  the two profiles are of different devices: /device:TPU:0 before, /device:TPU:8 now
where the time goes in v3:
time: 85.9 us; the launch traced here: 85.8 us
  Pallas kernels  77.8 us (91%)
  local copies, waits for them, and re-layouts  7.34 us (9%)
    pallas_call x1, Pallas kernels, exchange(): pl.pallas_call(functools.partial(exchange_kernel, tok, cap, top), out_sha...  77.8 us
    unnamed x5, local copies, waits for them, and re-layouts  7.34 us

profile of v3, /device:TPU:8, one launch (start us, length us, event | category | flops | bytes accessed | tf_op | source)
XLA Modules:
  0.0 85.8 jit_solution(16313907448695262643)
XLA Ops:
  0.6 77.8 %shard_map.146 = (bf16[128,1024]{1,0:T(8,128)(2,1)S(1)}, f32[8,128]{1,0:T(8,128)S(1)}, f32[2,1024,512]{2,1,0:T(8,128)S(1)}, f32[2,1024,512]{2,1,0:T(8,128)S(1)}, f32[2,512,1024]{2,1,0:T(8,128)S(1)}) custom-call(bf16[128,1024]{1,0:T(8,128)(2,1)} %dy_ref.1, s32[8,128]{1,0:T(8,128)} %bitcast.5, s32[8,128]{1,0:T(8,128)} %bitcast.6, f32[8,128]{1,0:T(8,128)} %bitcast.7, ...), custom_call_target="tpu_custom_call" | custom-call | tf_op jit(solution)/shard_map/pallas_call | solution.py:440
  78.4 0.7 copy.21
  79.1 0.6 copy.22
  79.7 2.0 %copy.23 = f32[2,1024,512]{2,1,0:T(8,128)} copy(f32[2,1024,512]{2,1,0:T(8,128)S(1)} %get-tuple-element.17) | data formatting | bytes 8388608
  81.7 2.0 %copy.24 = f32[2,1024,512]{2,1,0:T(8,128)} copy(f32[2,1024,512]{2,1,0:T(8,128)S(1)} %get-tuple-element.18) | data formatting | bytes 8388608
  83.7 2.0 %copy.25 = f32[2,512,1024]{2,1,0:T(8,128)} copy(f32[2,512,1024]{2,1,0:T(8,128)S(1)} %get-tuple-element.19) | data formatting | bytes 8388608
